TPU v7x, 32 devices: a whole 2x2x4 slice. The times are simulated.
32 devices in a mesh: cand: 4 (over x, core), tp: 8 (over z, y).
Axes of the slice: x: 2, y: 2, z: 4, core: 2. Of those that a mesh axis runs over, the one named last changes fastest.
Arguments:
- start_state: float32 [128], replicated, may hold values from -6 to 6
- goal: float32 [128], replicated, may hold values from -6 to 6
- mean_prev: float32 [128], replicated, may hold values from -0.5 to 0.5
- std_prev: float32 [128], replicated, may hold values from 0.1 to 0.5
- noise: float32 [768, 128], P('cand'), may hold values from -23 to 23
- members: int32 [768, 1], P('cand'), may hold values from 0 to 3; in each aligned block of 192 rows (0 to 191, 192 to 383, ...) at most 60 rows name the same one
- elites: int32 [96], replicated, may hold values from 0 to 767, as said below
- w_in: bfloat16 [4, 144, 4096], P(None, None, 'tp'), may hold values from -0.5 to 0.5
- w_hid: bfloat16 [4, 4096, 4096], P(None, None, 'tp'), may hold values from -0.09375 to 0.09375
- w_out: bfloat16 [4, 4096, 128], P(None, 'tp'), may hold values from -0.09375 to 0.09375
Outputs:
- scores: float32 [768], P('cand')
- new_mean: float32 [128], replicated
- new_std: float32 [128], replicated
Inputs may be any that keep to these rules, and one draw needn't show every extreme that they name: `members`: among the candidates of one index of cand no member is named more than 60 times. `elites`: 96 distinct candidate numbers.
All inputs are finite; a program needn't handle non-finite values.
Results may differ from a plain program's by a relative error of at most 0.0085.
Values may be sent and summed in bfloat16 or wider, within the bound.
A program may use at most 64 MiB of HBM per device.

v0:
```python
import jax
import jax.numpy as jnp
from jax import lax
from jax.sharding import PartitionSpec as P

HORIZON = 8


def reward_of(states, goal, action):
    return -jnp.mean((states - goal) ** 2, axis=-1) - 0.1 * jnp.mean(action * action, axis=-1)


def on_device(start_state, goal, mean_prev, std_prev, noise, members, elites, w_in, w_hid, w_out):
    local_count = noise.shape[0]
    member_count = w_in.shape[0]
    state_width = start_state.shape[0]
    capacity = 5 * local_count // 16
    action_width = mean_prev.shape[0] // HORIZON
    actions = mean_prev[None, :] + std_prev[None, :] * noise
    onehot = (members == jnp.arange(member_count, dtype=jnp.int32)[None, :]).astype(jnp.float32)
    before = jnp.cumsum(onehot, axis=0) - onehot
    position = jnp.sum(before * onehot, axis=1).astype(jnp.int32)
    slot_number = members[:, 0] * capacity + position
    dispatch = (
        slot_number[None, :] == jnp.arange(member_count * capacity, dtype=jnp.int32)[:, None]
    ).astype(jnp.float32)
    slot_actions = jnp.dot(dispatch, actions, precision=lax.Precision.HIGHEST)
    slot_actions = slot_actions.reshape(member_count, capacity, HORIZON, action_width)
    input_layer = lax.all_gather(w_in, "tp", axis=2, tiled=True)

    def rollout(first, count):
        layer_in = input_layer[first : first + count]
        hid_rows = w_hid[first : first + count]
        out_rows = w_out[first : first + count]
        states = jnp.zeros((count, capacity, state_width), jnp.float32) + start_state[None, None, :]
        running = jnp.zeros((count, capacity), jnp.float32)
        for step_index in range(HORIZON):
            action = slot_actions[first : first + count, :, step_index, :]
            inputs = jnp.concatenate([states, action], axis=2).astype(jnp.bfloat16)
            first_pre = jnp.einsum(
                "mck,mkh->mch", inputs, layer_in, preferred_element_type=jnp.float32
            )
            hidden_one = jax.nn.silu(first_pre).astype(jnp.bfloat16)
            second_pre = jnp.einsum(
                "mck,mkh->mch", hidden_one, hid_rows, preferred_element_type=jnp.float32
            )
            hidden_two = jax.nn.silu(second_pre).astype(jnp.bfloat16)
            partial_change = jnp.einsum(
                "mck,mks->mcs", hidden_two, out_rows, preferred_element_type=jnp.float32
            )
            change = lax.psum(partial_change, "tp")
            states = states + change
            running = running + reward_of(states, goal[None, None, :], action)
        return running

    slot_returns = jnp.concatenate([rollout(member, 1) for member in range(member_count)], axis=0)
    returns = jnp.dot(
        slot_returns.reshape(member_count * capacity), dispatch, precision=lax.Precision.HIGHEST
    )
    first_index = lax.axis_index("cand") * local_count
    numbers = first_index + jnp.arange(local_count, dtype=jnp.int32)
    chosen = jnp.sum((elites[:, None] == numbers[None, :]).astype(jnp.float32), axis=0)
    count_all = local_count * lax.axis_size("cand")
    return_sum = lax.psum(jnp.sum(returns), "cand")
    return_mean = return_sum / count_all
    return_spread = lax.psum(jnp.sum((returns - return_mean) ** 2), "cand")
    return_var = return_spread / count_all
    scores = (returns - return_mean) / jnp.sqrt(return_var + 1e-06)
    weights = chosen * (0.5 + jax.nn.sigmoid(scores))
    weight_sum, first_moment = lax.psum(
        (jnp.sum(weights), jnp.dot(weights, actions, precision=lax.Precision.HIGHEST)), "cand"
    )
    new_mean = first_moment / weight_sum
    action_spread = lax.psum(
        jnp.dot(weights, (actions - new_mean[None, :]) ** 2, precision=lax.Precision.HIGHEST),
        "cand",
    )
    new_var = action_spread / weight_sum
    new_std = jnp.sqrt(new_var + 1e-06)
    return (scores, new_mean, new_std)


def solution(mesh):
    placed = (
        P(),
        P(),
        P(),
        P(),
        P("cand", None),
        P("cand", None),
        P(),
        P(None, None, "tp"),
        P(None, None, "tp"),
        P(None, "tp", None),
    )
    return jax.shard_map(
        on_device, mesh=mesh, in_specs=placed, out_specs=(P("cand"), P(), P()), check_vma=False
    )
```

profile of v0, /device:TPU:0, one launch (start us, length us, event | category | flops | bytes accessed | tf_op | source)
XLA Modules:
  0.0 847.4 jit_solution(5525363201203804489)
XLA Ops:
  8.7 1.2 reduce-window.6
  16.0 77.4 %all-gather.2.cloned.1.call-done = bf16[4,144,4096]{2,1,0:T(8,128)(2,1)} async-done(((bf16[4,144,512]{2,1,0:T(8,128)(2,1)}), bf16[4,144,4096]{2,1,0:T(8,128)(2,1)}) %all-gather.2.cloned.1.call-update) | async-done | bytes 4718608 | tf_op jit(solution)/shard_map/all_gather | solution.py:29
  93.4 3.7 multiply_convert_fusion.109
  97.9 3.7 multiply_convert_fusion.133
  102.3 3.7 multiply_convert_fusion.157
  106.8 3.7 multiply_convert_fusion.85
  111.8 69.2 %all-reduce.33.cloned.1.call-done = (f32[1,60,128]{2,1,0:T(8,128)}, f32[1,60,128]{2,1,0:T(8,128)}, f32[1,60,128]{2,1,0:T(8,128)}, f32[1,60,128]{2,1,0:T(8,128)}) async-done(((f32[1,60,128]{2,1,0:T(8,128)}, f32[1,60,128]{2,1,0:T(8,128)}, f32[1,60,128]{2,1,0:T(8,128)}, f32[1,60,128]{2,1,0:T(8,128)}), (f32[1,60,128]{2,1,0:T(8,128)}, f32[1,60,128]{2,1,0:T(8,128)}, f32[1,60,128]{2,1,0:T(8,128)}, ...) | async-done | bytes 122896 | tf_op jit(solution)/shard_map/psum | solution.py:51
  181.7 3.7 multiply_convert_fusion.154
  186.2 3.7 multiply_convert_fusion.82
  190.7 3.7 multiply_convert_fusion.106
  195.1 3.7 multiply_convert_fusion.130
  200.4 69.7 %all-reduce.31.cloned.1.call-done = (f32[1,60,128]{2,1,0:T(8,128)}, f32[1,60,128]{2,1,0:T(8,128)}, f32[1,60,128]{2,1,0:T(8,128)}, f32[1,60,128]{2,1,0:T(8,128)}) async-done(((f32[1,60,128]{2,1,0:T(8,128)}, f32[1,60,128]{2,1,0:T(8,128)}, f32[1,60,128]{2,1,0:T(8,128)}, f32[1,60,128]{2,1,0:T(8,128)}), (f32[1,60,128]{2,1,0:T(8,128)}, f32[1,60,128]{2,1,0:T(8,128)}, f32[1,60,128]{2,1,0:T(8,128)}, ...) | async-done | bytes 122896 | tf_op jit(solution)/shard_map/psum | solution.py:51
  271.0 3.7 multiply_convert_fusion.151
  275.5 3.7 multiply_convert_fusion.79
  279.9 3.7 multiply_convert_fusion.103
  284.4 3.7 multiply_convert_fusion.127
  289.5 69.9 %all-reduce.29.cloned.1.call-done = (f32[1,60,128]{2,1,0:T(8,128)}, f32[1,60,128]{2,1,0:T(8,128)}, f32[1,60,128]{2,1,0:T(8,128)}, f32[1,60,128]{2,1,0:T(8,128)}) async-done(((f32[1,60,128]{2,1,0:T(8,128)}, f32[1,60,128]{2,1,0:T(8,128)}, f32[1,60,128]{2,1,0:T(8,128)}, f32[1,60,128]{2,1,0:T(8,128)}), (f32[1,60,128]{2,1,0:T(8,128)}, f32[1,60,128]{2,1,0:T(8,128)}, f32[1,60,128]{2,1,0:T(8,128)}, ...) | async-done | bytes 122896 | tf_op jit(solution)/shard_map/psum | solution.py:51
  360.2 3.7 multiply_convert_fusion.148
  364.7 3.7 multiply_convert_fusion.76
  369.2 3.7 multiply_convert_fusion.100
  373.6 3.7 multiply_convert_fusion.124
  378.8 69.9 %all-reduce.27.cloned.1.call-done = (f32[1,60,128]{2,1,0:T(8,128)}, f32[1,60,128]{2,1,0:T(8,128)}, f32[1,60,128]{2,1,0:T(8,128)}, f32[1,60,128]{2,1,0:T(8,128)}) async-done(((f32[1,60,128]{2,1,0:T(8,128)}, f32[1,60,128]{2,1,0:T(8,128)}, f32[1,60,128]{2,1,0:T(8,128)}, f32[1,60,128]{2,1,0:T(8,128)}), (f32[1,60,128]{2,1,0:T(8,128)}, f32[1,60,128]{2,1,0:T(8,128)}, f32[1,60,128]{2,1,0:T(8,128)}, ...) | async-done | bytes 122896 | tf_op jit(solution)/shard_map/psum | solution.py:51
  449.4 3.7 multiply_convert_fusion.145
  453.9 3.7 multiply_convert_fusion.73
  458.4 3.7 multiply_convert_fusion.97
  462.9 3.7 multiply_convert_fusion.121
  468.3 69.7 %all-reduce.25.cloned.1.call-done = (f32[1,60,128]{2,1,0:T(8,128)}, f32[1,60,128]{2,1,0:T(8,128)}, f32[1,60,128]{2,1,0:T(8,128)}, f32[1,60,128]{2,1,0:T(8,128)}) async-done(((f32[1,60,128]{2,1,0:T(8,128)}, f32[1,60,128]{2,1,0:T(8,128)}, f32[1,60,128]{2,1,0:T(8,128)}, f32[1,60,128]{2,1,0:T(8,128)}), (f32[1,60,128]{2,1,0:T(8,128)}, f32[1,60,128]{2,1,0:T(8,128)}, f32[1,60,128]{2,1,0:T(8,128)}, ...) | async-done | bytes 122896 | tf_op jit(solution)/shard_map/psum | solution.py:51
  538.7 3.7 multiply_convert_fusion.142
  543.2 3.7 multiply_convert_fusion.70
  547.7 3.7 multiply_convert_fusion.94
  552.2 3.7 multiply_convert_fusion.118
  557.2 70.0 %all-reduce.23.cloned.1.call-done = (f32[1,60,128]{2,1,0:T(8,128)}, f32[1,60,128]{2,1,0:T(8,128)}, f32[1,60,128]{2,1,0:T(8,128)}, f32[1,60,128]{2,1,0:T(8,128)}) async-done(((f32[1,60,128]{2,1,0:T(8,128)}, f32[1,60,128]{2,1,0:T(8,128)}, f32[1,60,128]{2,1,0:T(8,128)}, f32[1,60,128]{2,1,0:T(8,128)}), (f32[1,60,128]{2,1,0:T(8,128)}, f32[1,60,128]{2,1,0:T(8,128)}, f32[1,60,128]{2,1,0:T(8,128)}, ...) | async-done | bytes 122896 | tf_op jit(solution)/shard_map/psum | solution.py:51
  628.0 3.7 multiply_convert_fusion.139
  632.5 3.7 multiply_convert_fusion.67
  637.0 3.7 multiply_convert_fusion.91
  641.4 3.7 multiply_convert_fusion.115
  646.1 70.3 %all-reduce.21.cloned.1.call-done = (f32[1,60,128]{2,1,0:T(8,128)}, f32[1,60,128]{2,1,0:T(8,128)}, f32[1,60,128]{2,1,0:T(8,128)}, f32[1,60,128]{2,1,0:T(8,128)}) async-done(((f32[1,60,128]{2,1,0:T(8,128)}, f32[1,60,128]{2,1,0:T(8,128)}, f32[1,60,128]{2,1,0:T(8,128)}, f32[1,60,128]{2,1,0:T(8,128)}), (f32[1,60,128]{2,1,0:T(8,128)}, f32[1,60,128]{2,1,0:T(8,128)}, f32[1,60,128]{2,1,0:T(8,128)}, ...) | async-done | bytes 122896 | tf_op jit(solution)/shard_map/psum | solution.py:51
  717.2 3.7 multiply_convert_fusion.136
  721.7 3.7 multiply_convert_fusion.64
  726.2 3.7 multiply_convert_fusion.88
  730.7 3.7 multiply_convert_fusion.112
  735.2 70.5 %all-reduce.19.cloned.1.call-done = (f32[1,60,128]{2,1,0:T(8,128)}, f32[1,60,128]{2,1,0:T(8,128)}, f32[1,60,128]{2,1,0:T(8,128)}, f32[1,60,128]{2,1,0:T(8,128)}) async-done(((f32[1,60,128]{2,1,0:T(8,128)}, f32[1,60,128]{2,1,0:T(8,128)}, f32[1,60,128]{2,1,0:T(8,128)}, f32[1,60,128]{2,1,0:T(8,128)}), (f32[1,60,128]{2,1,0:T(8,128)}, f32[1,60,128]{2,1,0:T(8,128)}, f32[1,60,128]{2,1,0:T(8,128)}, ...) | async-done | bytes 122896 | tf_op jit(solution)/shard_map/psum | solution.py:51
  807.0 1.2 multiply_reduce_fusion.33
  809.2 6.3 psum.291
  816.8 7.2 psum.292
  826.1 6.6 all-reduce.9
  833.6 6.0 psum.295
  839.7 1.2 add_sqrt_fusion
  (209 shorter events, 46.9 us)
Async XLA Ops:
  7.2 86.2 %all-gather.2.cloned.1.call-start = ((), (), s32[]{:S(2)}) async-start(), calls=%async_computation | async-start | bytes 5308416 | tf_op jit(solution)/shard_map/all_gather | solution.py:29
  7.9 173.0 %all-reduce.33.cloned.1.call-start = ((), (), s32[]{:S(2)}) async-start(), calls=%async_computation.8 | async-start | bytes 262144 | tf_op jit(solution)/shard_map/psum | solution.py:51
  93.4 3.7 copy-start
  106.8 74.1 %copy-start.22 = (f32[128]{0:T(128)S(1)}, f32[128]{0:T(128)}, u32[]{:S(2)}) copy-start(f32[128]{0:T(128)} %param.10) | copy-start | bytes 1540
  111.3 158.8 %all-reduce.31.cloned.1.call-start = ((), (), s32[]{:S(2)}) async-start(), calls=%async_computation.7 | async-start | bytes 262144 | tf_op jit(solution)/shard_map/psum | solution.py:51
  195.1 75.0 %copy-start.2 = (f32[1,60,128]{2,1,0:T(8,128)S(1)}, f32[1,60,128]{2,1,0:T(8,128)}, u32[]{:S(2)}) copy-start(f32[1,60,128]{2,1,0:T(8,128)} %get-tuple-element.73) | copy-start | bytes 92164
  195.1 75.0 %copy-start.3 = (f32[1,60,128]{2,1,0:T(8,128)S(1)}, f32[1,60,128]{2,1,0:T(8,128)}, u32[]{:S(2)}) copy-start(f32[1,60,128]{2,1,0:T(8,128)} %get-tuple-element.74) | copy-start | bytes 92164
  195.1 75.0 %copy-start.4 = (f32[1,60,128]{2,1,0:T(8,128)S(1)}, f32[1,60,128]{2,1,0:T(8,128)}, u32[]{:S(2)}) copy-start(f32[1,60,128]{2,1,0:T(8,128)} %get-tuple-element.75) | copy-start | bytes 92164
  195.1 75.0 %copy-start.5 = (f32[1,60,128]{2,1,0:T(8,128)S(1)}, f32[1,60,128]{2,1,0:T(8,128)}, u32[]{:S(2)}) copy-start(f32[1,60,128]{2,1,0:T(8,128)} %get-tuple-element.76) | copy-start | bytes 92164
  199.6 159.8 %all-reduce.29.cloned.1.call-start = ((), (), s32[]{:S(2)}) async-start(), calls=%async_computation.6 | async-start | bytes 262144 | tf_op jit(solution)/shard_map/psum | solution.py:51
  288.9 159.8 %all-reduce.27.cloned.1.call-start = ((), (), s32[]{:S(2)}) async-start(), calls=%async_computation.5 | async-start | bytes 262144 | tf_op jit(solution)/shard_map/psum | solution.py:51
  360.2 4.5 copy-start.12
  360.2 4.5 copy-start.13
  378.1 159.8 %all-reduce.25.cloned.1.call-start = ((), (), s32[]{:S(2)}) async-start(), calls=%async_computation.4 | async-start | bytes 262144 | tf_op jit(solution)/shard_map/psum | solution.py:51
  449.4 4.5 copy-start.17
  453.9 4.5 copy-start.11
  458.4 4.5 copy-start.8
  467.4 159.8 %all-reduce.23.cloned.1.call-start = ((), (), s32[]{:S(2)}) async-start(), calls=%async_computation.3 | async-start | bytes 262144 | tf_op jit(solution)/shard_map/psum | solution.py:51
  538.7 4.5 copy-start.15
  543.2 4.5 copy-start.9
  547.7 4.5 copy-start.6
  556.7 159.7 %all-reduce.21.cloned.1.call-start = ((), (), s32[]{:S(2)}) async-start(), calls=%async_computation.2 | async-start | bytes 262144 | tf_op jit(solution)/shard_map/psum | solution.py:51
  628.0 4.5 copy-start.16
  632.5 4.5 copy-start.10
  637.0 4.5 copy-start.7
  645.9 159.8 %all-reduce.19.cloned.1.call-start = ((), (), s32[]{:S(2)}) async-start(), calls=%async_computation.1 | async-start | bytes 262144 | tf_op jit(solution)/shard_map/psum | solution.py:51
  717.2 4.5 copy-start.19
  721.7 4.5 copy-start.18
  726.2 4.5 copy-start.14
  730.7 75.1 %copy-start.23 = (f32[128]{0:T(128)S(1)}, f32[128]{0:T(128)}, u32[]{:S(2)}) copy-start(f32[128]{0:T(128)} %param.11) | copy-start | bytes 1540
  730.7 86.1 %copy-start.25 = (s32[96]{0:T(128)S(1)}, s32[96]{0:T(128)}, u32[]{:S(2)}) copy-start(s32[96]{0:T(128)} %param.16) | copy-start | bytes 1156
  730.7 95.3 %copy-start.1 = (f32[192,128]{1,0:T(8,128)S(1)}, f32[192,128]{1,0:T(8,128)}, u32[]{:S(2)}) copy-start(f32[192,128]{1,0:T(8,128)} %param.14) | copy-start | bytes 294916
  730.7 95.2 %copy-start.20 = (f32[128]{0:T(128)S(1)}, f32[128]{0:T(128)}, u32[]{:S(2)}) copy-start(f32[128]{0:T(128)} %param.13) | copy-start | bytes 1540
  730.7 95.2 %copy-start.21 = (f32[128]{0:T(128)S(1)}, f32[128]{0:T(128)}, u32[]{:S(2)}) copy-start(f32[128]{0:T(128)} %param.12) | copy-start | bytes 1540
  833.4 7.4 copy-start.24
Sparse Core Ops, SparseCore 0:
  10.0 83.3 all-gather.1
  111.4 69.4 all-reduce.32
  199.8 70.3 all-reduce.30
  289.0 70.3 all-reduce.28
  378.3 70.3 all-reduce.26
  467.5 70.4 all-reduce.24
  556.8 70.3 all-reduce.22
  646.1 70.3 all-reduce.20
  735.4 70.3 all-reduce.18
where the time goes:
time: 849 us; the launch traced here: 847 us
  waiting for transfers between devices  637 us (75%)
  matrix products  144 us (17%)
  blocking collectives  26.2 us (3%)
  other arithmetic  19 us (2%)
  between operations  15.8 us (2%)
    psum x8, waiting for transfers between devices, rollout(): change = lax.psum(partial_change, 'tp')  559 us
    dot_general x32, matrix products, rollout(): jnp.einsum('mck,mkh->mch', hidden_one, hid_rows, preferred_element_type=j...  118 us
    all_gather x1, waiting for transfers between devices, on_device(): input_layer = lax.all_gather(w_in, 'tp', axis=2, tiled=True)  77.4 us
    dot_general x32, matrix products, rollout(): jnp.einsum('mck,mks->mcs', hidden_two, out_rows, preferred_element_type=j...  24.4 us
  transfers between devices with their start and end apart: 9, of which 9 were waited for; matrix products, arithmetic and copies ran while one was open for 1% of the time, Pallas kernels for 0%

commit v1 on v0

v1 whole, which is shorter than its diff:
```python
import functools
import jax
import jax.numpy as jnp
from jax import lax
from jax.experimental import pallas as pl
from jax.experimental.pallas import tpu as pltpu
from jax.sharding import PartitionSpec as P

HORIZON = 8
F32 = jnp.float32
BF16 = jnp.bfloat16
HI = lax.Precision.HIGHEST


def silu(v):
    h = 0.5 * v
    return h + h * jnp.tanh(h)


def kernel(
    n_cand, n_tp, cap,
    start_ref, goal_ref, mean_ref, std_ref, noise_ref, members_ref, elites_ref,
    win_hbm, whid_hbm, wout_hbm,
    scores_ref, new_mean_ref, new_std_ref,
    win_v, whid_v, wout_v, h1_v, pf, ps, rs_rx, xs, xs_send, state, sq, big,
    act_send, act_rx, act_t, sa_all, meta_all, ret_all,
    load_sem, win_s, win_r, act_s, act_r, sa_s, sa_r, meta_s, meta_r,
    rs_s, rs_r, ag_s, ag_r, ret_s, ret_r,
):
    n_mem = win_hbm.shape[0]
    chunk = win_hbm.shape[2]
    width = start_ref.shape[1]
    local = noise_ref.shape[0]
    rows = n_mem * cap
    own = rows // n_tp
    a_dim = mean_ref.shape[1] // HORIZON
    c = lax.axis_index("cand")
    t = lax.axis_index("tp")
    m = lax.rem(c, n_mem)
    group = c - m

    def tp_peer(d):
        return lax.rem(t + d, n_tp)

    def remote(src, dst, s, r, cc, tt):
        return pltpu.make_async_remote_copy(
            src_ref=src, dst_ref=dst, send_sem=s, recv_sem=r,
            device_id={"cand": cc, "tp": tt}, device_id_type=pl.DeviceIdType.MESH,
        )

    win_copies = [
        remote(win_hbm.at[m], win_v.at[d], win_s.at[d], win_r.at[d], c, tp_peer(d))
        for d in range(1, n_tp)
    ]
    for cp in win_copies:
        cp.start()
    loads = [pltpu.make_async_copy(win_hbm.at[m], win_v.at[0], load_sem.at[n_tp])]
    for d in range(n_tp):
        src = lax.rem(t + n_tp - d, n_tp)
        loads.append(pltpu.make_async_copy(
            whid_hbm.at[m, pl.ds(pl.multiple_of(src * chunk, chunk), chunk), :],
            whid_v.at[pl.ds(d * chunk, chunk), :], load_sem.at[d]))
    loads.append(pltpu.make_async_copy(wout_hbm.at[m], wout_v, load_sem.at[n_tp + 1]))
    for cp in loads:
        cp.start()

    actions = mean_ref[...] + std_ref[...] * noise_ref[...]
    members = members_ref[...]
    lane = lax.broadcasted_iota(jnp.int32, (local, 128), 1)
    onehot = (members == lane).astype(F32)
    lower = (
        lax.broadcasted_iota(jnp.int32, (local, local), 1)
        < lax.broadcasted_iota(jnp.int32, (local, local), 0)
    ).astype(BF16)
    before = jnp.dot(lower, onehot.astype(BF16), preferred_element_type=F32)
    position = jnp.sum(before * onehot, axis=1, keepdims=True).astype(jnp.int32)
    slot = members * cap + position
    place = slot == lax.broadcasted_iota(jnp.int32, (local, rows), 1)
    place_f = place.astype(F32)
    over_cands = (((0,), (0,)), ((), ()))
    act_send[...] = lax.dot_general(
        place_f.astype(BF16), actions.astype(BF16), over_cands, preferred_element_type=F32
    ).astype(BF16)
    mine = pl.multiple_of(m * cap, cap)
    act_copies = []
    for k in range(1, n_mem):
        m2 = lax.rem(m + k, n_mem)
        act_copies.append(remote(
            act_send.at[pl.ds(pl.multiple_of(m2 * cap, cap), cap), :],
            act_rx.at[pl.ds(mine, cap), :], act_s.at[k], act_r.at[k], group + m2, t))
    for cp in act_copies:
        cp.start()
    act_rx[pl.ds(mine, cap), :] = act_send[pl.ds(mine, cap), :]

    numbers = c * local + lax.broadcasted_iota(jnp.int32, (local, 1), 0)
    chosen = jnp.sum((numbers == elites_ref[...]).astype(F32), axis=1, keepdims=True)
    action_cost = jnp.sum(actions * actions, axis=1, keepdims=True) * (0.1 / a_dim)
    facts = jnp.where(lane == 0, 1.0, jnp.where(lane == 1, chosen, jnp.where(lane == 2, action_cost, 0.0)))
    sa_all[c] = lax.dot_general(place_f, actions, over_cands, precision=HI, preferred_element_type=F32)
    meta_all[c] = lax.dot_general(facts, place_f, over_cands, precision=HI, preferred_element_type=F32)[:8]
    side_copies = []
    for k in range(1, n_cand):
        c2 = lax.rem(c + k, n_cand)
        side_copies.append(remote(meta_all.at[c], meta_all.at[c], meta_s.at[k], meta_r.at[k], c2, t))
        side_copies.append(remote(sa_all.at[c], sa_all.at[c], sa_s.at[k], sa_r.at[k], c2, t))
    for cp in side_copies:
        cp.start()

    state[...] = jnp.broadcast_to(start_ref[...], state.shape)
    sq[...] = jnp.zeros_like(sq)
    xs[...] = jnp.broadcast_to(start_ref[...], xs.shape).astype(BF16)
    for cp in act_copies:
        cp.wait_recv()
    for s in range(HORIZON):
        act_t[s] = act_rx[...].astype(F32)[:, s * a_dim:(s + 1) * a_dim].astype(BF16)
    for cp in loads:
        cp.wait()
    for cp in win_copies:
        cp.wait_recv()

    half = min(256, chunk)
    first_own = pl.multiple_of(t * own, own)

    def step_body(step, carry):
        x = jnp.concatenate([xs[...], act_t[step]], axis=1)
        for d in range(n_tp):
            h1_v[:, d * chunk:(d + 1) * chunk] = silu(
                jnp.dot(x, win_v[d], preferred_element_type=F32)).astype(BF16)
        total = None
        for n in range(chunk // half):
            h2 = silu(jnp.dot(h1_v[...], whid_v[:, n * half:(n + 1) * half],
                              preferred_element_type=F32)).astype(BF16)
            part = jnp.dot(h2, wout_v[n * half:(n + 1) * half, :], preferred_element_type=F32)
            total = part if total is None else total + part
        pf[...] = total
        ps[...] = total.astype(BF16)
        rs = [
            remote(ps.at[pl.ds(pl.multiple_of(tp_peer(d) * own, own), own), :], rs_rx.at[d],
                   rs_s.at[d], rs_r.at[d], c, tp_peer(d))
            for d in range(1, n_tp)
        ]
        for cp in rs:
            cp.start()
        change = pf[pl.ds(first_own, own), :]
        for d in range(1, n_tp):
            rs[d - 1].wait_recv()
            change = change + rs_rx[d].astype(F32)
        new_state = state[...] + change
        state[...] = new_state
        ag = [
            remote(xs_send, xs.at[pl.ds(first_own, own), :], ag_s.at[d], ag_r.at[d], c, tp_peer(d))
            for d in range(1, n_tp)
        ]

        @pl.when(step < HORIZON - 1)
        def _():
            xs_send[...] = new_state.astype(BF16)
            for cp in ag:
                cp.start()
            xs[pl.ds(first_own, own), :] = new_state.astype(BF16)

        gap = new_state - goal_ref[...]
        sq[...] += gap * gap
        for cp in rs:
            cp.wait_send()

        @pl.when(step < HORIZON - 1)
        def _():
            for cp in ag:
                cp.wait()

        return carry

    lax.fori_loop(0, HORIZON, step_body, 0)

    big[...] = jnp.zeros_like(big)
    big[pl.ds(pl.multiple_of(m * cap + lax.rem(t * own, cap), own), own), :] = sq[...] * (1.0 / width)
    row = lax.dot_general(jnp.ones((8, width), F32), big[...], (((1,), (1,)), ((), ())),
                          precision=HI, preferred_element_type=F32)
    me = c * n_tp + t
    ret_all[me] = row[0:1]
    ret_copies = []
    for kc in range(n_cand):
        for kt in range(n_tp):
            if kc + kt:
                i = kc * n_tp + kt
                ret_copies.append(remote(ret_all.at[me], ret_all.at[me], ret_s.at[i], ret_r.at[i],
                                         lax.rem(c + kc, n_cand), tp_peer(kt)))
    for cp in ret_copies:
        cp.start()
    for cp in side_copies:
        cp.wait_recv()
    for cp in ret_copies:
        cp.wait_recv()

    per_block = cap // own
    returns = []
    for b in range(n_cand):
        parts = [ret_all[(b - b % n_mem + m2) * n_tp + b % n_mem * per_block + h]
                 for m2 in range(n_mem) for h in range(per_block)]
        returns.append(-functools.reduce(jnp.add, parts) - meta_all[b, 2:3, :])
    count = local * n_cand

    def over(vals):
        return jnp.sum(functools.reduce(jnp.add, vals), axis=1, keepdims=True)

    valid = [meta_all[b, 0:1, :] for b in range(n_cand)]
    mean = over([valid[b] * returns[b] for b in range(n_cand)]) / count
    var = over([valid[b] * (returns[b] - mean) ** 2 for b in range(n_cand)]) / count
    scale = jnp.sqrt(var + 1e-06)
    scores = [(returns[b] - mean) / scale for b in range(n_cand)]
    weights = [meta_all[b, 1:2, :] * (0.5 + 1.0 / (1.0 + jnp.exp(-scores[b]))) for b in range(n_cand)]
    weight_sum = over(weights)

    def moment(values):
        rows8 = [jnp.broadcast_to(weights[b], (8, rows)) for b in range(n_cand)]
        return functools.reduce(jnp.add, [
            jnp.dot(rows8[b], values(b), precision=HI, preferred_element_type=F32)
            for b in range(n_cand)])[0:1] / weight_sum

    new_mean = moment(lambda b: sa_all[b])
    new_mean_ref[...] = new_mean
    new_std_ref[...] = jnp.sqrt(moment(lambda b: (sa_all[b] - new_mean) ** 2) + 1e-06)

    my_parts = [ret_all[(group + m2) * n_tp + m * per_block + h]
                for m2 in range(n_mem) for h in range(per_block)]
    my_returns = -functools.reduce(jnp.add, my_parts) - meta_all[c, 2:3, :]
    my_scores = jnp.broadcast_to((my_returns - mean) / scale, (8, rows))
    scores_ref[...] = lax.dot_general(my_scores, place_f, (((1,), (1,)), ((), ())),
                                      precision=HI, preferred_element_type=F32)[0:1]

    for cp in win_copies + act_copies + side_copies + ret_copies:
        cp.wait_send()


def on_device(n_cand, n_tp, start_state, goal, mean_prev, std_prev, noise, members, elites, w_in, w_hid, w_out):
    local = noise.shape[0]
    n_mem, depth, chunk = w_in.shape
    width = start_state.shape[0]
    flat = mean_prev.shape[0]
    hidden = w_hid.shape[1]
    cap = -(-(5 * local // 16) // 16) * 16
    rows = n_mem * cap
    own = rows // n_tp
    total = n_cand * n_tp
    vmem = pl.BlockSpec(memory_space=pltpu.VMEM)
    hbm = pl.BlockSpec(memory_space=pl.ANY)
    dma = pltpu.SemaphoreType.DMA
    scores, new_mean, new_std = pl.pallas_call(
        functools.partial(kernel, n_cand, n_tp, cap),
        out_shape=(
            jax.ShapeDtypeStruct((1, local), F32),
            jax.ShapeDtypeStruct((1, flat), F32),
            jax.ShapeDtypeStruct((1, flat), F32),
        ),
        in_specs=[vmem] * 7 + [hbm] * 3,
        out_specs=(vmem,) * 3,
        scratch_shapes=[
            pltpu.VMEM((n_tp, depth, chunk), BF16),
            pltpu.VMEM((hidden, chunk), BF16),
            pltpu.VMEM((chunk, width), BF16),
            pltpu.VMEM((rows, hidden), BF16),
            pltpu.VMEM((rows, width), F32),
            pltpu.VMEM((rows, width), BF16),
            pltpu.VMEM((n_tp, own, width), BF16),
            pltpu.VMEM((rows, width), BF16),
            pltpu.VMEM((own, width), BF16),
            pltpu.VMEM((own, width), F32),
            pltpu.VMEM((own, width), F32),
            pltpu.VMEM((rows, width), F32),
            pltpu.VMEM((rows, flat), BF16),
            pltpu.VMEM((rows, flat), BF16),
            pltpu.VMEM((HORIZON, rows, flat // HORIZON), BF16),
            pltpu.VMEM((n_cand, rows, flat), F32),
            pltpu.VMEM((n_cand, 8, rows), F32),
            pltpu.VMEM((total, 1, rows), F32),
            dma((n_tp + 2,)),
            dma((n_tp,)), dma((n_tp,)),
            dma((n_mem,)), dma((n_mem,)),
            dma((n_cand,)), dma((n_cand,)),
            dma((n_cand,)), dma((n_cand,)),
            dma((n_tp,)), dma((n_tp,)),
            dma((n_tp,)), dma((n_tp,)),
            dma((total,)), dma((total,)),
        ],
        compiler_params=pltpu.CompilerParams(has_side_effects=True, vmem_limit_bytes=56 << 20),
    )(
        start_state.reshape(1, -1), goal.reshape(1, -1), mean_prev.reshape(1, -1),
        std_prev.reshape(1, -1), noise, members, elites.reshape(1, -1), w_in, w_hid, w_out,
    )
    return scores.reshape(-1), new_mean.reshape(-1), new_std.reshape(-1)


def solution(mesh):
    placed = (
        P(), P(), P(), P(), P("cand", None), P("cand", None), P(),
        P(None, None, "tp"), P(None, None, "tp"), P(None, "tp", None),
    )
    return jax.shard_map(
        functools.partial(on_device, mesh.shape["cand"], mesh.shape["tp"]),
        mesh=mesh, in_specs=placed, out_specs=(P("cand"), P(), P()), check_vma=False,
    )
```

time: 849 us -> 132 us (0.16)
  waiting for transfers between devices: 637 us -> 0 us
  matrix products: 144 us -> 0 us
  Pallas kernels: 0 us -> 126 us
  blocking collectives: 26.2 us -> 0 us
  other arithmetic: 19 us -> 0 us
  between operations: 15.8 us -> 0.64 us
    psum x8 -> x0, waiting for transfers between devices: 559 us -> none  [rollout(): change = lax.psum(partial_change, 'tp')]
    dot_general x68 -> x0, matrix products: 144 us -> none  [the longest x32 118 us: rollout(): jnp.einsum('mck,mkh->mch', hidden_one, hid_rows, preferred_element_type=j...]
    pallas_call x0 -> x1, Pallas kernels: none -> 126 us  [on_device(): pl.pallas_call(functools.partial(kernel, n_cand, n_tp, cap), out_shape=(j...]
    all_gather x1 -> x0, waiting for transfers between devices: 77.4 us -> none  [on_device(): input_layer = lax.all_gather(w_in, 'tp', axis=2, tiled=True)]
    psum x4 -> x0, blocking collectives: 26.2 us -> none  [the longest x1 7.24 us: on_device(): return_spread = lax.psum(jnp.sum((returns - return_mean) ** 2), 'cand')]
  transfers between devices with their start and end apart: 9 -> 0, of which waited for: 9 -> 0; matrix products, arithmetic and copies ran while one was open for 1% -> 0% of each run, Pallas kernels for 0% -> 0%
where the time goes in v1:
time: 132 us
  Pallas kernels  126 us (95%)
  local copies, waits for them, and re-layouts  4.96 us (4%)
    pallas_call x1, Pallas kernels, on_device(): pl.pallas_call(functools.partial(kernel, n_cand, n_tp, cap), out_shape=(j...  126 us
    unnamed x4, local copies, waits for them, and re-layouts  4.96 us

profile of v1, /device:TPU:0, one launch (start us, length us, event | category | flops | bytes accessed | tf_op | source)
XLA Modules:
  0.0 131.9 jit_solution(7455275371884563805)
XLA Ops:
  0.6 1.4 %copy.13.members_ref = s32[192,1]{1,0:T(8,128)} copy(s32[192,1]{0,1:T(1,128)} %param.15) | data formatting | bytes 1536 | tf_op args[5]
  2.1 126.3 %shard_map.121 = (f32[1,192]{1,0:T(1,128)}, f32[1,128]{1,0:T(1,128)}, f32[1,128]{1,0:T(1,128)}) custom-call(f32[1,128]{1,0:T(1,128)} %bitcast.9, f32[1,128]{1,0:T(1,128)} %bitcast.10, f32[1,128]{1,0:T(1,128)} %bitcast.11, f32[1,128]{1,0:T(1,128)} %bitcast.12, f32[192,128]{1,0:T(8,128)} %noise_ref.1, s32[192,1]{1,0:T(8,128)} %copy.13.members_ref, ...), custom_call_target="tpu_custom_call" | custom-call | tf_op jit(solution)/shard_map/pallas_call | solution.py:249
  128.4 1.2 copy.17
  129.7 1.1 copy.18
  130.8 1.2 copy.19

commit v2 on v1

--- a/solution.py
+++ b/solution.py
@@ -32,7 +32,10 @@
     width = start_ref.shape[1]
     local = noise_ref.shape[0]
     rows = n_mem * cap
-    own = rows // n_tp
+    lowest = n_tp // 4
+    owners = range(lowest, n_tp - lowest)
+    n_own = len(owners)
+    own = rows // n_own
     a_dim = mean_ref.shape[1] // HORIZON
     c = lax.axis_index("cand")
     t = lax.axis_index("tp")
@@ -48,19 +51,23 @@
             device_id={"cand": cc, "tp": tt}, device_id_type=pl.DeviceIdType.MESH,
         )
 
+    pair = t + 1 - 2 * lax.rem(t, 2)
     win_copies = [
-        remote(win_hbm.at[m], win_v.at[d], win_s.at[d], win_r.at[d], c, tp_peer(d))
-        for d in range(1, n_tp)
+        remote(win_hbm.at[m], win_v.at[t], win_s.at[d], win_r.at[t], c, pair if d == 1 else tp_peer(d))
+        for d in [1] + list(range(2, n_tp, 2))
     ]
     for cp in win_copies:
         cp.start()
-    loads = [pltpu.make_async_copy(win_hbm.at[m], win_v.at[0], load_sem.at[n_tp])]
-    for d in range(n_tp):
+
+    def arrived(d):
         src = lax.rem(t + n_tp - d, n_tp)
-        loads.append(pltpu.make_async_copy(
-            whid_hbm.at[m, pl.ds(pl.multiple_of(src * chunk, chunk), chunk), :],
-            whid_v.at[pl.ds(d * chunk, chunk), :], load_sem.at[d]))
-    loads.append(pltpu.make_async_copy(wout_hbm.at[m], wout_v, load_sem.at[n_tp + 1]))
+        return remote(win_hbm.at[m], win_v.at[src], win_s.at[0], win_r.at[src], c, pair)
+
+    loads = [
+        pltpu.make_async_copy(win_hbm.at[m], win_v.at[t], load_sem.at[0]),
+        pltpu.make_async_copy(whid_hbm.at[m], whid_v, load_sem.at[1]),
+    ]
+    loads.append(pltpu.make_async_copy(wout_hbm.at[m], wout_v, load_sem.at[2]))
     for cp in loads:
         cp.start()
 
@@ -115,88 +122,116 @@
         act_t[s] = act_rx[...].astype(F32)[:, s * a_dim:(s + 1) * a_dim].astype(BF16)
     for cp in loads:
         cp.wait()
-    for cp in win_copies:
-        cp.wait_recv()
+    for d in range(2, n_tp, 2):
+        arrived(d).wait_recv()
+        src = lax.rem(t + n_tp - d, n_tp)
+        cp = remote(win_v.at[src], win_v.at[src], win_s.at[d + 1], win_r.at[src], c, pair)
+        cp.start()
+        win_copies.append(cp)
+    for d in range(1, n_tp, 2):
+        arrived(d).wait_recv()
 
     half = min(256, chunk)
-    first_own = pl.multiple_of(t * own, own)
+    owner = jnp.logical_and(t >= owners[0], t <= owners[-1])
+    place_own = t - lowest
+    first_own = pl.multiple_of(place_own * own, own)
 
     def step_body(step, carry):
-        x = jnp.concatenate([xs[...], act_t[step]], axis=1)
-        for d in range(n_tp):
-            h1_v[:, d * chunk:(d + 1) * chunk] = silu(
-                jnp.dot(x, win_v[d], preferred_element_type=F32)).astype(BF16)
-        total = None
-        for n in range(chunk // half):
-            h2 = silu(jnp.dot(h1_v[...], whid_v[:, n * half:(n + 1) * half],
-                              preferred_element_type=F32)).astype(BF16)
-            part = jnp.dot(h2, wout_v[n * half:(n + 1) * half, :], preferred_element_type=F32)
-            total = part if total is None else total + part
-        pf[...] = total
-        ps[...] = total.astype(BF16)
         rs = [
-            remote(ps.at[pl.ds(pl.multiple_of(tp_peer(d) * own, own), own), :], rs_rx.at[d],
-                   rs_s.at[d], rs_r.at[d], c, tp_peer(d))
-            for d in range(1, n_tp)
+            remote(ps.at[pl.ds(i * own, own), :], rs_rx.at[t], rs_s.at[i], rs_r.at[t], c, o)
+            for i, o in enumerate(owners)
         ]
-        for cp in rs:
+        for q in range(2):
+            lo, hi = q * rows // 2, (q + 1) * rows // 2
+            held = range(q * n_own // 2, (q + 1) * n_own // 2)
+
+            @pl.when(step > 0)
+            def _():
+                for i in held:
+                    pl.when(t != owners[i])(remote(
+                        xs_send, xs.at[pl.ds(i * own, own), :], ag_s.at[0], ag_r.at[i], c, pair).wait_recv)
+
+            x = jnp.concatenate([xs[lo:hi, :], act_t[step, lo:hi, :]], axis=1)
+            for d in range(n_tp):
+                h1_v[lo:hi, d * chunk:(d + 1) * chunk] = silu(
+                    jnp.dot(x, win_v[d], preferred_element_type=F32)).astype(BF16)
+            total = None
+            for n in range(chunk // half):
+                h2 = silu(jnp.dot(h1_v[lo:hi, :], whid_v[:, n * half:(n + 1) * half],
+                                  preferred_element_type=F32)).astype(BF16)
+                part = jnp.dot(h2, wout_v[n * half:(n + 1) * half, :], preferred_element_type=F32)
+                total = part if total is None else total + part
+            pf[lo:hi, :] = total
+            ps[lo:hi, :] = total.astype(BF16)
+            for i in held:
+                pl.when(t != owners[i])(rs[i].start)
+
+        @pl.when(owner)
+        def _():
+            change = pf[pl.ds(first_own, own), :]
+            for d in range(1, n_tp):
+                src = lax.rem(t + n_tp - d, n_tp)
+                remote(ps.at[pl.ds(0, own), :], rs_rx.at[src], rs_s.at[0], rs_r.at[src], c, pair).wait_recv()
+                change = change + rs_rx[src].astype(F32)
+            new_state = state[...] + change
+            state[...] = new_state
+
+            ag = [
+                remote(xs_send, xs.at[pl.ds(first_own, own), :], ag_s.at[d], ag_r.at[place_own], c, tp_peer(d))
+                for d in range(1, n_tp)
+            ]
+
+            @pl.when(step < HORIZON - 1)
+            def _():
+                xs_send[...] = new_state.astype(BF16)
+                for cp in ag:
+                    cp.start()
+                xs[pl.ds(first_own, own), :] = new_state.astype(BF16)
+
+            gap = new_state - goal_ref[...]
+            sq[...] += gap * gap
+
+            @pl.when(step < HORIZON - 1)
+            def _():
+                for cp in ag:
+                    cp.wait_send()
+
+        for o, cp in zip(owners, rs):
+            pl.when(t != o)(cp.wait_send)
+
+        return carry
+
+    lax.fori_loop(0, HORIZON, step_body, 0)
+
+    me = c * n_own + place_own
+    ret_copies = [
+        remote(ret_all.at[me], ret_all.at[me], ret_s.at[kc * n_tp + kt], ret_r.at[me],
+               lax.rem(c + kc, n_cand), tp_peer(kt))
+        for kc in range(n_cand) for kt in range(n_tp) if kc + kt
+    ]
+
+    @pl.when(owner)
+    def _():
+        big[...] = jnp.zeros_like(big)
+        big[pl.ds(pl.multiple_of(m * cap + lax.rem(first_own, cap), own), own), :] = sq[...] * (1.0 / width)
+        row = lax.dot_general(jnp.ones((8, width), F32), big[...], (((1,), (1,)), ((), ())),
+                              precision=HI, preferred_element_type=F32)
+        ret_all[me] = row[0:1]
+        for cp in ret_copies:
             cp.start()
-        change = pf[pl.ds(first_own, own), :]
-        for d in range(1, n_tp):
-            rs[d - 1].wait_recv()
-            change = change + rs_rx[d].astype(F32)
-        new_state = state[...] + change
-        state[...] = new_state
-        ag = [
-            remote(xs_send, xs.at[pl.ds(first_own, own), :], ag_s.at[d], ag_r.at[d], c, tp_peer(d))
-            for d in range(1, n_tp)
-        ]
-
-        @pl.when(step < HORIZON - 1)
-        def _():
-            xs_send[...] = new_state.astype(BF16)
-            for cp in ag:
-                cp.start()
-            xs[pl.ds(first_own, own), :] = new_state.astype(BF16)
-
-        gap = new_state - goal_ref[...]
-        sq[...] += gap * gap
-        for cp in rs:
-            cp.wait_send()
-
-        @pl.when(step < HORIZON - 1)
-        def _():
-            for cp in ag:
-                cp.wait()
-
-        return carry
-
-    lax.fori_loop(0, HORIZON, step_body, 0)
-
-    big[...] = jnp.zeros_like(big)
-    big[pl.ds(pl.multiple_of(m * cap + lax.rem(t * own, cap), own), own), :] = sq[...] * (1.0 / width)
-    row = lax.dot_general(jnp.ones((8, width), F32), big[...], (((1,), (1,)), ((), ())),
-                          precision=HI, preferred_element_type=F32)
-    me = c * n_tp + t
-    ret_all[me] = row[0:1]
-    ret_copies = []
-    for kc in range(n_cand):
-        for kt in range(n_tp):
-            if kc + kt:
-                i = kc * n_tp + kt
-                ret_copies.append(remote(ret_all.at[me], ret_all.at[me], ret_s.at[i], ret_r.at[i],
-                                         lax.rem(c + kc, n_cand), tp_peer(kt)))
-    for cp in ret_copies:
-        cp.start()
+
     for cp in side_copies:
         cp.wait_recv()
-    for cp in ret_copies:
-        cp.wait_recv()
+    for cc in range(n_cand):
+        for i, o in enumerate(owners):
+            k = cc * n_own + i
+            pl.when(jnp.logical_or(t != o, c != cc))(remote(
+                ret_all.at[k], ret_all.at[k], ret_s.at[0], ret_r.at[k], c, pair).wait_recv)
 
     per_block = cap // own
     returns = []
     for b in range(n_cand):
-        parts = [ret_all[(b - b % n_mem + m2) * n_tp + b % n_mem * per_block + h]
+        parts = [ret_all[(b - b % n_mem + m2) * n_own + b % n_mem * per_block + h]
                  for m2 in range(n_mem) for h in range(per_block)]
         returns.append(-functools.reduce(jnp.add, parts) - meta_all[b, 2:3, :])
     count = local * n_cand
@@ -222,15 +257,20 @@
     new_mean_ref[...] = new_mean
     new_std_ref[...] = jnp.sqrt(moment(lambda b: (sa_all[b] - new_mean) ** 2) + 1e-06)
 
-    my_parts = [ret_all[(group + m2) * n_tp + m * per_block + h]
+    my_parts = [ret_all[(group + m2) * n_own + m * per_block + h]
                 for m2 in range(n_mem) for h in range(per_block)]
     my_returns = -functools.reduce(jnp.add, my_parts) - meta_all[c, 2:3, :]
     my_scores = jnp.broadcast_to((my_returns - mean) / scale, (8, rows))
     scores_ref[...] = lax.dot_general(my_scores, place_f, (((1,), (1,)), ((), ())),
                                       precision=HI, preferred_element_type=F32)[0:1]
 
-    for cp in win_copies + act_copies + side_copies + ret_copies:
+    for cp in win_copies + act_copies + side_copies:
         cp.wait_send()
+
+    @pl.when(owner)
+    def _():
+        for cp in ret_copies:
+            cp.wait_send()
 
 
 def on_device(n_cand, n_tp, start_state, goal, mean_prev, std_prev, noise, members, elites, w_in, w_hid, w_out):
@@ -241,7 +281,8 @@
     hidden = w_hid.shape[1]
     cap = -(-(5 * local // 16) // 16) * 16
     rows = n_mem * cap
-    own = rows // n_tp
+    n_own = n_tp - 2 * (n_tp // 4)
+    own = rows // n_own
     total = n_cand * n_tp
     vmem = pl.BlockSpec(memory_space=pltpu.VMEM)
     hbm = pl.BlockSpec(memory_space=pl.ANY)
@@ -273,8 +314,8 @@
             pltpu.VMEM((HORIZON, rows, flat // HORIZON), BF16),
             pltpu.VMEM((n_cand, rows, flat), F32),
             pltpu.VMEM((n_cand, 8, rows), F32),
-            pltpu.VMEM((total, 1, rows), F32),
-            dma((n_tp + 2,)),
+            pltpu.VMEM((n_cand * n_own, 1, rows), F32),
+            dma((3,)),
             dma((n_tp,)), dma((n_tp,)),
             dma((n_mem,)), dma((n_mem,)),
             dma((n_cand,)), dma((n_cand,)),

time: 132 us -> 116 us (0.88)
  Pallas kernels: 126 us -> 110 us
    pallas_call x1, Pallas kernels: 126 us -> 110 us  [on_device(): pl.pallas_call(functools.partial(kernel, n_cand, n_tp, cap), out_shape=(j...]
where the time goes in v2:
time: 116 us
  Pallas kernels  110 us (95%)
  local copies, waits for them, and re-layouts  4.96 us (4%)
    pallas_call x1, Pallas kernels, on_device(): pl.pallas_call(functools.partial(kernel, n_cand, n_tp, cap), out_shape=(j...  110 us
    unnamed x4, local copies, waits for them, and re-layouts  4.96 us

profile of v2, /device:TPU:0, one launch (start us, length us, event | category | flops | bytes accessed | tf_op | source)
XLA Modules:
  0.0 115.9 jit_solution(10298567908774377290)
XLA Ops:
  0.6 1.4 %copy.13.members_ref = s32[192,1]{1,0:T(8,128)} copy(s32[192,1]{0,1:T(1,128)} %param.15) | data formatting | bytes 1536 | tf_op args[5]
  2.1 110.3 %shard_map.121 = (f32[1,192]{1,0:T(1,128)}, f32[1,128]{1,0:T(1,128)}, f32[1,128]{1,0:T(1,128)}) custom-call(f32[1,128]{1,0:T(1,128)} %bitcast.9, f32[1,128]{1,0:T(1,128)} %bitcast.10, f32[1,128]{1,0:T(1,128)} %bitcast.11, f32[1,128]{1,0:T(1,128)} %bitcast.12, f32[192,128]{1,0:T(8,128)} %noise_ref.1, s32[192,1]{1,0:T(8,128)} %copy.13.members_ref, ...), custom_call_target="tpu_custom_call" | custom-call | tf_op jit(solution)/shard_map/pallas_call | solution.py:290
  112.4 1.2 %copy.17 = f32[192]{0:T(256)} copy(f32[192]{0:T(256)} %bitcast.8) | data formatting | bytes 1536
  113.6 1.1 copy.18
  114.7 1.2 %copy.19 = f32[128]{0:T(128)} copy(f32[128]{0:T(128)} %bitcast.14) | data formatting | bytes 1024
